TPU v7x, 256 devices: a whole 4x4x8 slice. The times are simulated.
256 devices in a mesh: dp: 64 (over z, x, core), tensor: 4 (over y).
Axes of the slice: x: 4, y: 4, z: 8, core: 2. Of those that a mesh axis runs over, the one named last changes fastest.
Arguments:
- queries: bfloat16 [2048, 32, 2048], P('dp', None, 'tensor'), may hold values from -8 to 8
- keys: bfloat16 [2048, 32, 512], P('dp', None, 'tensor'), may hold values from -8 to 8
- values: bfloat16 [2048, 32, 512], P('dp', None, 'tensor'), may hold values from -6 to 6
- out_weight: bfloat16 [2048, 4096], P(None, 'tensor'), may hold values from -0.125 to 0.125
- dest_slot: int32 [2048], P('dp'), may hold values from 0 to 63, as said below
- pack_slot: int32 [64, 32], P('dp'), may hold values from 0 to 63, as said below
- seq_start: int32 [64, 32], P('dp'), may hold values from 0 to 1024, as said below
- seq_len: int32 [64, 32], P('dp'), may hold values from 0 to 1024, as said below
Outputs:
- projected: bfloat16 [2048, 32, 4096], P('dp', None, 'tensor')
Inputs may be any that keep to these rules, and one draw needn't show every extreme that they name: Block i of loader l goes to pack dest_slot[l * 32 + i]; the 32 values of one loader are distinct. pack_slot[p, s] = l + m names the block of loader l whose dest_slot is p + m; the values of one pack are distinct, and every block of every loader fills exactly one position of one pack, so each pack holds exactly 32 blocks. Multiples of 32; seq_start[p, 0] = 0, the used entries rise, and a sequence's blocks run up to the next used start (or to the pack's end); the entries after the used ones equal 1024. Some pack holds a single sequence of all its blocks. `seq_len`: for a used sequence of b blocks, from b * 32 - 32 // 4 + 1 to b * 32; 0 for unused entries.
All inputs are finite; a program needn't handle non-finite values.
Results may differ from a plain program's by a relative error of at most 0.01.
Values may be sent and summed in bfloat16 or wider, within the bound.
A program may use at most 64 MiB of HBM per device.

v0:
```python
import jax
import jax.numpy as jnp
from jax import lax
from jax.sharding import PartitionSpec as P

HEAD_SIZE = 128


def sent_together(arrays, axis, split_dim, concat_dim, along):
    ends, at = ([], 0)
    for a in arrays[:-1]:
        at += a.shape[along]
        ends.append(at)
    both = jnp.concatenate(arrays, axis=along)
    return tuple(
        jnp.split(
            lax.all_to_all(both, axis, split_axis=split_dim, concat_axis=concat_dim, tiled=True),
            ends,
            axis=along,
        )
    )


def tile_scores(query_tile, key_tile, score_scale):
    return (
        jnp.einsum("rgnd,cgd->gnrc", query_tile, key_tile, preferred_element_type=jnp.float32)
        * score_scale
    )


def tile_mix(weight_tile, value_tile):
    return jnp.einsum("gnrc,cgd->rgnd", weight_tile, value_tile, preferred_element_type=jnp.float32)


def attend(packed_queries, packed_keys, packed_values, starts, lengths, block_rows):
    total_row_count, query_cols = packed_queries.shape
    kv_heads = packed_keys.shape[1] // HEAD_SIZE
    query_group_count = query_cols // HEAD_SIZE // kv_heads
    tile_rows = 16 * block_rows
    score_scale = 1.0 / HEAD_SIZE**0.5
    row_ids = jnp.arange(total_row_count, dtype=jnp.int32)
    segment = jnp.sum((starts[None, :] <= row_ids[:, None]).astype(jnp.int32), axis=1) - 1
    picked = segment[:, None] == jnp.arange(starts.shape[0], dtype=jnp.int32)[None, :]
    begins = jnp.sum(jnp.where(picked, starts[None, :], 0), axis=1)
    limits = jnp.sum(jnp.where(picked, lengths[None, :], 0), axis=1)
    usable = row_ids - begins < limits
    query_head_rows = packed_queries.reshape(
        total_row_count, kv_heads, query_group_count, HEAD_SIZE
    )
    key_head_rows = packed_keys.reshape(total_row_count, kv_heads, HEAD_SIZE)
    value_head_rows = packed_values.reshape(total_row_count, kv_heads, HEAD_SIZE)
    blocks_out = []
    for tile_index in range(total_row_count // tile_rows):
        first_row = tile_index * tile_rows
        end_row = first_row + tile_rows
        query_tile = query_head_rows[first_row:end_row]
        score_tiles = []
        needed_flags = []
        for key_index in range(tile_index + 1):
            key_first = key_index * tile_rows
            key_tile = key_head_rows[key_first : key_first + tile_rows]
            needed = jnp.array(True)
            scores = tile_scores(query_tile, key_tile, score_scale)
            score_tiles.append(scores)
            needed_flags.append(needed)
        scores = jnp.concatenate(score_tiles, axis=-1)
        allowed = (segment[first_row:end_row, None] == segment[None, :end_row]) & (
            row_ids[None, :end_row] <= row_ids[first_row:end_row, None]
        )
        scores = jnp.where(allowed[None, None], scores, -jnp.inf)
        largest = jnp.max(scores, axis=-1, keepdims=True)
        exponent = jnp.exp(scores - largest)
        weights = (exponent / jnp.sum(exponent, axis=-1, keepdims=True)).astype(jnp.bfloat16)
        mixture = jnp.zeros((tile_rows, kv_heads, query_group_count, HEAD_SIZE), jnp.float32)
        for key_index in range(tile_index + 1):
            key_first = key_index * tile_rows
            weight_tile = weights[..., key_first : key_first + tile_rows]
            value_tile = value_head_rows[key_first : key_first + tile_rows]
            part_sum = tile_mix(weight_tile, value_tile)
            mixture = mixture + part_sum
        mixture = jnp.where(usable[first_row:end_row, None, None, None], mixture, 0.0)
        blocks_out.append(mixture.reshape(tile_rows, query_cols).astype(jnp.bfloat16))
    return jnp.concatenate(blocks_out, axis=0)


def body(queries, keys, values, out_weight, dest_slot, pack_slot, seq_start, seq_len):
    local_blocks, block_rows, query_cols = queries.shape
    loaders = lax.axis_size("dp")
    capacity = (local_blocks + loaders - 1) // loaders
    slot_count = loaders * capacity

    def outgoing(portion):
        return (
            jnp.zeros((slot_count,) + portion.shape[1:], portion.dtype).at[dest_slot].set(portion)
        )

    arrived = sent_together((outgoing(queries), outgoing(keys), outgoing(values)), "dp", 0, 0, 2)
    sources = pack_slot[0]

    def collect(portion):
        return jnp.take(portion, sources, axis=0).reshape(
            local_blocks * block_rows, portion.shape[2]
        )

    attended = attend(
        collect(arrived[0]),
        collect(arrived[1]),
        collect(arrived[2]),
        seq_start[0],
        seq_len[0],
        block_rows,
    )
    going_back = (
        jnp.zeros((slot_count, block_rows, query_cols), jnp.bfloat16)
        .at[sources]
        .set(attended.reshape(local_blocks, block_rows, query_cols))
    )
    returned = lax.all_to_all(going_back, "dp", split_axis=0, concat_axis=0, tiled=True)
    own_rows = jnp.take(returned, dest_slot, axis=0).reshape(local_blocks * block_rows, query_cols)
    projected = jnp.dot(
        lax.all_gather(own_rows, "tensor", axis=1, tiled=True),
        out_weight,
        preferred_element_type=jnp.float32,
    )
    return projected.astype(jnp.bfloat16).reshape(local_blocks, block_rows, out_weight.shape[1])


def solution(mesh):
    placed = (
        P("dp", None, "tensor"),
        P("dp", None, "tensor"),
        P("dp", None, "tensor"),
        P(None, "tensor"),
        P("dp"),
        P("dp", None),
        P("dp", None),
        P("dp", None),
    )
    return jax.shard_map(
        body, mesh=mesh, in_specs=placed, out_specs=P("dp", None, "tensor"), check_vma=False
    )
```

profile of v0, /device:TPU:1, one launch (start us, length us, event | category | flops | bytes accessed | tf_op | source)
XLA Modules:
  0.0 252.0 jit_solution(6751222511268654765)
XLA Ops:
  6.5 0.7 compare_select_fusion
  7.3 0.2 broadcast.198.clone
  7.5 3.6 %scatter_fusion = bf16[64,32,512]{2,1,0:T(8,128)(2,1)S(1)} fusion(bf16[64,32,512]{2,1,0:T(8,128)(2,1)S(1)} %broadcast.198.clone, s32[32]{0:T(128)S(1)} %compare_select_fusion, bf16[32,32,512]{2,1,0:T(8,128)(2,1)} %param.12), kind=kCustom, calls=%fused_computation.4 | custom fusion | bytes 3145856 | tf_op jit(solution)/shard_map/scatter | solution.py:94
  11.1 0.1 broadcast.204.clone.1
  11.2 1.5 scatter_fusion.1
  12.7 0.1 broadcast.204.clone
  12.8 0.0 copy-done.4
  12.8 1.5 scatter_fusion.2
  14.3 2.0 pad_maximum_fusion
  16.4 13.1 %all-to-all-start = ((bf16[64,32,768]{2,1,0:T(8,128)(2,1)}), bf16[64,32,768]{2,1,0:T(8,128)(2,1)S(1)}, u32[]{:S(2)}, u32[]{:S(2)}) async-start(bf16[64,32,768]{2,1,0:T(8,128)(2,1)} %pad_maximum_fusion), calls=%async_computation | async-start | bytes 6291456 | tf_op jit(solution)/shard_map/all_to_all | solution.py:17
  29.6 0.1 convert_reduce_fusion
  29.7 0.1 select_reduce_fusion.1
  29.9 0.3 compare_and_fusion
  30.1 1.2 fusion.8
  31.4 70.5 %all-to-all-done = bf16[64,32,768]{2,1,0:T(8,128)(2,1)S(1)} async-done(((bf16[64,32,768]{2,1,0:T(8,128)(2,1)}), bf16[64,32,768]{2,1,0:T(8,128)(2,1)S(1)}, u32[]{:S(2)}, u32[]{:S(2)}) %all-to-all-start) | async-done | bytes 3145760 | tf_op jit(solution)/shard_map/all_to_all | solution.py:17
  101.9 1.1 fusion.30
  103.1 2.3 gather_fusion
  105.4 2.3 gather_fusion.1
  107.7 1.5 split.14
  109.2 2.3 gather_fusion.2
  111.5 0.2 broadcast_select_fusion.1
  111.7 0.1 fusion.31
  111.8 0.1 reshape.323
  111.9 0.1 broadcast_select_fusion.2
  112.1 0.9 fusion.3
  113.0 0.9 fusion.2
  113.9 1.4 fusion.18
  115.3 0.2 copy.32
  115.6 0.1 reshape.325
  115.7 0.7 multiply_bitcast_fusion.1
  116.4 0.7 multiply_bitcast_fusion
  117.1 1.2 fusion.1
  118.4 1.6 fusion
  119.9 1.8 divide_convert_fusion
  121.7 0.5 fusion.4
  122.2 0.5 fusion.22
  122.7 0.2 copy.33
  122.9 0.1 pad_maximum_fusion.1
  123.0 1.6 broadcast.198
  124.5 4.6 %scatter_fusion.3 = bf16[64,32,512]{2,1,0:T(8,128)(2,1)} fusion(bf16[64,32,512]{2,1,0:T(8,128)(2,1)} %broadcast.198, s32[32]{0:T(128)S(1)} %fusion.27, bf16[32,32,512]{2,1,0:T(8,128)(2,1)S(1)} %bitcast.103), kind=kCustom, calls=%fused_computation.7 | custom fusion | bytes 3145856 | tf_op jit(solution)/shard_map/scatter | solution.py:116
  129.1 6.7 %all-to-all-start.1 = ((bf16[64,32,512]{2,1,0:T(8,128)(2,1)}), bf16[64,32,512]{2,1,0:T(8,128)(2,1)S(1)}, u32[]{:S(2)}, u32[]{:S(2)}) async-start(bf16[64,32,512]{2,1,0:T(8,128)(2,1)} %scatter_fusion.3), calls=%async_computation.1 | async-start | bytes 4194304 | tf_op jit(solution)/shard_map/all_to_all | solution.py:118
  135.8 0.3 all-gather.2.cloned.1.call-start
  136.1 49.4 %all-to-all-done.1 = bf16[64,32,512]{2,1,0:T(8,128)(2,1)S(1)} async-done(((bf16[64,32,512]{2,1,0:T(8,128)(2,1)}), bf16[64,32,512]{2,1,0:T(8,128)(2,1)S(1)}, u32[]{:S(2)}, u32[]{:S(2)}) %all-to-all-start.1) | async-done | bytes 2097184 | tf_op jit(solution)/shard_map/all_to_all | solution.py:118
  185.5 0.6 gather_fusion.3
  186.1 1.1 broadcast_select_fusion
  187.3 0.0 all-gather.2.cloned.1.call-update
  187.3 48.5 %all-gather.2.cloned.1.call-done = bf16[1024,2048]{1,0:T(8,128)(2,1)} async-done(((bf16[1024,512]{1,0:T(8,128)(2,1)}), bf16[1024,2048]{1,0:T(8,128)(2,1)}) %all-gather.2.cloned.1.call-update) | async-done | bytes 4194320 | tf_op jit(solution)/shard_map/all_gather | solution.py:121
  235.8 9.3 %convolution_convert_fusion = bf16[1024,1024]{1,0:T(8,128)(2,1)} fusion(bf16[1024,2048]{1,0:T(8,128)(2,1)} %all-gather.2.cloned.1.call-done, bf16[2048,1024]{1,0:T(8,128)(2,1)} %param.15), kind=kOutput, calls=%fused_computation.30 | convolution fusion | flops 4296015872 | bytes 10485760 | tf_op jit(solution)/shard_map/dot_general | solution.py:120
  (32 shorter events, 0.1 us)
Async XLA Ops:
  6.5 4.6 %copy-start.3 = (bf16[32,32,128]{2,1,0:T(8,128)(2,1)S(1)}, bf16[32,32,128]{2,1,0:T(8,128)(2,1)}, u32[]{:S(2)}) copy-start(bf16[32,32,128]{2,1,0:T(8,128)(2,1)} %param.13) | copy-start | bytes 786436
  6.5 6.3 %copy-start.4 = (bf16[32,32,128]{2,1,0:T(8,128)(2,1)S(1)}, bf16[32,32,128]{2,1,0:T(8,128)(2,1)}, u32[]{:S(2)}) copy-start(bf16[32,32,128]{2,1,0:T(8,128)(2,1)} %param.14) | copy-start | bytes 786436
  16.4 13.2 %copy-start.7 = (s32[1,32]{1,0:T(1,128)S(1)}, s32[1,32]{1,0:T(1,128)}, u32[]{:S(2)}) copy-start(s32[1,32]{1,0:T(1,128)} %param.17) | copy-start | bytes 388
  16.4 13.2 %copy-start.5 = (s32[1,32]{1,0:T(1,128)S(1)}, s32[1,32]{1,0:T(1,128)}, u32[]{:S(2)}) copy-start(s32[1,32]{1,0:T(1,128)} %param.18) | copy-start | bytes 388
  16.4 13.3 %copy-start.6 = (s32[1,32]{1,0:T(1,128)S(1)}, s32[1,32]{1,0:T(1,128)}, u32[]{:S(2)}) copy-start(s32[1,32]{1,0:T(1,128)} %param.19) | copy-start | bytes 388
  16.4 85.5 %all-to-all-start = ((bf16[64,32,768]{2,1,0:T(8,128)(2,1)}), bf16[64,32,768]{2,1,0:T(8,128)(2,1)S(1)}, u32[]{:S(2)}, u32[]{:S(2)}) async-start(bf16[64,32,768]{2,1,0:T(8,128)(2,1)} %pad_maximum_fusion), calls=%async_computation | async-start | bytes 6291456 | tf_op jit(solution)/shard_map/all_to_all | solution.py:17
  109.2 2.7 %copy-start.1 = (bf16[32,32,128]{2,1,0:T(8,128)(2,1)S(1)}, bf16[32,32,128]{2,1,0:T(8,128)(2,1)}, u32[]{:S(2)}) copy-start(bf16[32,32,128]{2,1,0:T(8,128)(2,1)} %gather_fusion) | copy-start | bytes 786436
  109.2 2.7 %copy-start.2 = (bf16[32,32,128]{2,1,0:T(8,128)(2,1)S(1)}, bf16[32,32,128]{2,1,0:T(8,128)(2,1)}, u32[]{:S(2)}) copy-start(bf16[32,32,128]{2,1,0:T(8,128)(2,1)} %gather_fusion.1) | copy-start | bytes 786436
  115.7 1.4 copy-start
  124.5 11.6 %copy-start.8 = (s32[32]{0:T(128)S(1)}, s32[32]{0:T(128)}, u32[]{:S(2)}) copy-start(s32[32]{0:T(128)} %param.16) | copy-start | bytes 388
  129.1 56.4 %all-to-all-start.1 = ((bf16[64,32,512]{2,1,0:T(8,128)(2,1)}), bf16[64,32,512]{2,1,0:T(8,128)(2,1)S(1)}, u32[]{:S(2)}, u32[]{:S(2)}) async-start(bf16[64,32,512]{2,1,0:T(8,128)(2,1)} %scatter_fusion.3), calls=%async_computation.1 | async-start | bytes 4194304 | tf_op jit(solution)/shard_map/all_to_all | solution.py:118
  135.8 100.0 %all-gather.2.cloned.1.call-start = ((), (), s32[]{:S(2)}) async-start(), calls=%async_computation.2 | async-start | bytes 5242880 | tf_op jit(solution)/shard_map/all_gather | solution.py:121
Sparse Core Ops, SparseCore 0:
  187.4 48.3 all-gather.1
where the time goes:
time: 253 us; the launch traced here: 252 us
  waiting for transfers between devices  168 us (66%)
  local copies, waits for them, and re-layouts  24.2 us (10%)
  starting transfers between devices  20.1 us (8%)
  matrix products  14 us (6%)
  between operations  13.8 us (5%)
  other arithmetic  11.5 us (5%)
    all_to_all x1, waiting for transfers between devices, sent_together(): lax.all_to_all(both, axis, split_axis=split_dim, concat_axis=concat_dim,...  70.5 us
    all_to_all x1, waiting for transfers between devices, body(): lax.all_to_all(going_back, 'dp', split_axis=0, concat_axis=0, tiled=True)  49.4 us
    all_gather x1, waiting for transfers between devices, body(): lax.all_gather(own_rows, 'tensor', axis=1, tiled=True)  48.5 us
    all_to_all x1, starting transfers between devices, sent_together(): lax.all_to_all(both, axis, split_axis=split_dim, concat_axis=concat_dim,...  13.1 us
    dot_general x1, matrix products, body(): jnp.dot(lax.all_gather(own_rows, 'tensor', axis=1, tiled=True), out_weigh...  9.27 us
    gather x3, local copies, waits for them, and re-layouts, collect(): jnp.take(portion, sources, axis=0)  6.9 us
    all_to_all x1, starting transfers between devices, body(): lax.all_to_all(going_back, 'dp', split_axis=0, concat_axis=0, tiled=True)  6.71 us
    scatter x3, local copies, waits for them, and re-layouts, outgoing(): jnp.zeros((slot_count,) + portion.shape[1:], portion.dtype).at[dest_slot]  6.62 us
  transfers between devices with their start and end apart: 3, of which 3 were waited for; matrix products, arithmetic and copies ran while one was open for 1% of the time, Pallas kernels for 0%

commit v1 on v0

v1 whole, which is shorter than its diff:
```python
import functools

import jax
import jax.numpy as jnp
from jax import lax
from jax.experimental import pallas as pl
from jax.experimental.pallas import tpu as pltpu
from jax.sharding import PartitionSpec as P

MESH = pl.DeviceIdType.MESH
HEAD_SIZE = 128
NZ, NX, NC, NY = 8, 4, 2, 4
BLOCKS, ROWS, COLS = 32, 32, 512
GROUP = 256
HALF = 128
NEG = -1e30
FAR = 1 << 20
LOG2E = 1.4426950408889634


def lookup_tables(dest_slot, pack_slot, seq_start, seq_len):
    mine = jnp.concatenate([dest_slot, pack_slot[0], seq_start[0], seq_len[0]])
    table = lax.all_gather(mine, "dp")
    me = lax.axis_index("dp")
    z, x, c = me // (NX * NC), (me // NC) % NX, me % NC
    count = jnp.arange(BLOCKS, dtype=jnp.int32)
    dest, sources = table[:, :32], table[:, 32:64]
    query_loader = (z * NX + (x + jnp.arange(NX)) % NX) * NC + c
    pack = jnp.take(dest, query_loader, axis=0).reshape(-1)
    rows = jnp.take(table, pack, axis=0)
    loader = jnp.repeat(query_loader, BLOCKS)[:, None]
    place = jnp.sum(jnp.where(rows[:, 32:64] == loader, count, 0), axis=1)
    starts = rows[:, 64:96]
    begin = jnp.max(jnp.where(starts <= place[:, None] * ROWS, starts, 0), axis=1)
    length = jnp.sum(jnp.where(starts == begin[:, None], rows[:, 96:], 0), axis=1)
    left = begin + length - place * ROWS
    key_z = jnp.tile((z + jnp.arange(NZ)) % NZ, NC)
    key_c = jnp.repeat((c + jnp.arange(NC)) % NC, NZ)
    key_loader = (key_z * NX + x) * NC + key_c
    found = sources[:, None, :] == key_loader[None, :, None]
    position = jnp.sum(jnp.where(found, count, 0), axis=2)
    position = jnp.where(jnp.any(found, axis=2), position * ROWS, FAR)
    key_row = (position[:, :, None] + jnp.arange(ROWS, dtype=jnp.int32)).reshape(N_PACKS, NC * NZ * ROWS)
    packs = jnp.arange(N_PACKS, dtype=jnp.int32)
    held = jnp.take(dest, key_loader, axis=0)[None] == packs[:, None, None]
    block = jnp.sum(jnp.where(held, count, 0), axis=2)
    query_table = jnp.concatenate([pack, place, begin, left[:BLOCKS]]).astype(jnp.int32)
    return query_table, block.reshape(-1).astype(jnp.int32), key_row.astype(jnp.int32)


N_PACKS = NZ * NX * NC


def heads_down(tile):
    return jnp.concatenate([tile[:, h * HEAD_SIZE : (h + 1) * HEAD_SIZE] for h in range(4)], axis=0)


def heads_across(tile):
    return jnp.concatenate([tile[h * ROWS : (h + 1) * ROWS] for h in range(4)], axis=1)


def diagonal():
    shape = (HEAD_SIZE, HEAD_SIZE)
    return lax.broadcasted_iota(jnp.int32, shape, 0) == lax.broadcasted_iota(jnp.int32, shape, 1)


def merge(parts):
    top = functools.reduce(jnp.maximum, [s for _, s in parts])
    shares = [jnp.exp2(s - top) for _, s in parts]
    total = functools.reduce(jnp.add, shares)
    shares = [s / total for s in shares]
    eye = diagonal()
    merged = []
    for b in range(4):
        weights = jnp.concatenate(
            [jnp.where(eye, s[b : b + 1], 0.0).astype(jnp.bfloat16) for s in shares], axis=1
        )
        outputs = jnp.concatenate([heads_down(o[b * ROWS : (b + 1) * ROWS]) for o, _ in parts], axis=0)
        merged.append(heads_across(jnp.dot(weights, outputs, preferred_element_type=jnp.float32)))
    return merged, top + jnp.log2(total)


def kernel(
    query_table, block_table, key_row, queries, keys, values, weight, projected,
    kv, qx, att, lse, early, early_lse, late, late_lse, own, w, out,
    local_sem, z_send, z_recv, core_send, core_recv, x_send, x_recv,
    early_send, early_recv, early_lse_send, early_lse_recv,
    late_send, late_recv, late_lse_send, late_lse_recv,
    y_send, y_recv, y2_send, y2_recv, out_sem,
):
    me, y = lax.axis_index("dp"), lax.axis_index("tensor")
    z, x, c = me // (NX * NC), (me // NC) % NX, me % NC

    def at(z, x, c):
        return ((z * NX + x) * NC + c, y)

    z_near = [at((z + 1) % NZ, x, c), at((z + NZ - 1) % NZ, x, c)]
    x_near = [at(z, (x + 1) % NX, c), at(z, (x + NX - 1) % NX, c)]
    y_near = [(me, (y + 1) % NY), (me, (y + NY - 1) % NY)]
    partner = at(z, x, 1 - c)

    def remote(src, dst, send, recv, device):
        return pltpu.make_async_remote_copy(
            src_ref=src, dst_ref=dst, send_sem=send, recv_sem=recv, device_id=device, device_id_type=MESH
        )

    loads = [
        pltpu.make_async_copy(keys, kv.at[0, 0, 0], local_sem.at[0]),
        pltpu.make_async_copy(values, kv.at[0, 0, 1], local_sem.at[1]),
        pltpu.make_async_copy(queries, qx.at[0], local_sem.at[2]),
    ]
    for load in loads:
        load.start()
    weight_load = pltpu.make_async_copy(weight, w, local_sem.at[3])
    weight_load.start()

    barrier = pltpu.get_barrier_semaphore()
    for device in z_near + x_near + y_near + [partner]:
        pl.semaphore_signal(barrier, inc=1, device_id=device, device_id_type=MESH)
    pl.semaphore_wait(barrier, 7)
    for load in loads:
        load.wait()

    started = []

    def start(copy):
        copy.start()
        started.append(copy)

    def z_copy(way, hop, t):
        src = (NZ - hop) % NZ if way == 0 else hop
        dst = NZ - hop - 1 if way == 0 else hop + 1
        return remote(
            kv.at[0, src, t], kv.at[0, dst, t], z_send.at[way, hop, t], z_recv.at[way, hop, t], z_near[way]
        )

    def z_goes(way, hop, t):
        return hop < 3 or (hop == 3 and t == way)

    def core_copy(d, t):
        return remote(kv.at[0, d, t], kv.at[1, d, t], core_send.at[d, t], core_recv.at[d, t], partner)

    def x_copy(way, n):
        g = n if n < 4 else n - 4 + 2 * way
        src, dst = (0, 3 - 2 * way) if n < 4 else (3 - 2 * way, 2)
        rows = pl.ds(g * GROUP, GROUP)
        return remote(qx.at[src, rows], qx.at[dst, rows], x_send.at[way, n], x_recv.at[way, n], x_near[way])

    for t in range(2):
        for way in range(2):
            start(z_copy(way, 0, t))
    for n in range(4):
        for way in range(2):
            start(x_copy(way, n))
    for t in range(2):
        start(core_copy(0, t))

    for hop in range(4):
        for t in range(2):
            for way in range(2):
                if not z_goes(way, hop, t):
                    continue
                z_copy(way, hop, t).wait_recv()
                if z_goes(way, hop + 1, t):
                    start(z_copy(way, hop + 1, t))
                start(core_copy(NZ - hop - 1 if way == 0 else hop + 1, t))
            n = 2 * hop + t
            if n < 4:
                for way in range(2):
                    x_copy(way, n).wait_recv()
                    if n // 2 == way:
                        start(x_copy(way, 4 + n % 2))
            elif n < 6:
                for way in range(2):
                    x_copy(way, n).wait_recv()
    for d in range(NZ):
        for t in range(2):
            core_copy(d, t).wait_recv()

    scale = LOG2E / HEAD_SIZE**0.5

    def attend_four(r, g, half):
        base = pl.multiple_of(g * GROUP + half * HALF, HALF)
        eye = diagonal()
        row_in_block = lax.broadcasted_iota(jnp.int32, (4 * ROWS, 1), 0) % ROWS
        sums = []
        for b in range(4):
            n = r * BLOCKS + g * 8 + half * 4 + b
            pack, place, begin = query_table[n], query_table[128 + n], query_table[256 + n]
            rows = pl.ds(base + b * ROWS, ROWS)
            q = heads_down(qx[r, rows, :])
            at_block = [block_table[pack * 16 + j] for j in range(16)]
            key_tile = jnp.concatenate([kv[j // NZ, j % NZ, 0, at_block[j]] for j in range(16)], axis=0)
            value_tile = jnp.concatenate([kv[j // NZ, j % NZ, 1, at_block[j]] for j in range(16)], axis=0)
            scores = lax.dot_general(
                q, key_tile, (((1,), (1,)), ((), ())), preferred_element_type=jnp.float32
            )
            key_at = key_row[pl.ds(pack, 1), :]
            key_at = jnp.where(key_at >= begin, key_at, FAR)
            scores = jnp.where(key_at <= place * ROWS + row_in_block, scores * scale, NEG)
            top = jnp.max(scores, axis=1, keepdims=True)
            terms = jnp.exp2(scores - top)
            total = jnp.sum(terms, axis=1, keepdims=True)
            mixed = jnp.dot(terms.astype(jnp.bfloat16), value_tile, preferred_element_type=jnp.float32)
            att[r, rows, :] = heads_across(mixed / total).astype(jnp.bfloat16)
            sums.append(jnp.sum(jnp.where(eye, top + jnp.log2(total), 0.0), axis=0, keepdims=True))
        lse[r, g, half] = jnp.concatenate(sums + [jnp.zeros((4, HEAD_SIZE), jnp.float32)], axis=0)

    def attend(g, first, last):
        def step(u, carry):
            v = u // 2
            attend_four((6 - v) % 4, g + (3 - v) // 3, u % 2)
            return carry

        lax.fori_loop(first, last, step, 0)

    def early_copies(g, way):
        rows = pl.ds(g * GROUP + way * HALF, HALF)
        return [
            remote(
                att.at[2, rows], early.at[way, g], early_send.at[way, g], early_recv.at[way, g], x_near[way]
            ),
            remote(
                lse.at[2, g, way], early_lse.at[way, g],
                early_lse_send.at[way, g], early_lse_recv.at[way, g], x_near[way],
            ),
        ]

    def late_copies(g, way, half):
        r = 1 + 2 * way
        rows = pl.ds(g * GROUP + half * HALF, HALF)
        return [
            remote(
                att.at[r, rows], late.at[way, rows],
                late_send.at[way, g, half], late_recv.at[way, g, half], x_near[way],
            ),
            remote(
                lse.at[r, g, half], late_lse.at[way, g, half],
                late_lse_send.at[way, g, half], late_lse_recv.at[way, g, half], x_near[way],
            ),
        ]

    def y_copy(g, way):
        rows = pl.ds(g * GROUP, GROUP)
        return remote(
            own.at[0, rows], own.at[3 - 2 * way, rows], y_send.at[way, g], y_recv.at[way, g], y_near[way]
        )

    def y2_copy(g, way):
        rows = pl.ds(g * GROUP + way * HALF, HALF)
        return remote(
            own.at[3 - 2 * way, rows], own.at[2, rows], y2_send.at[way, g], y2_recv.at[way, g], y_near[way]
        )

    def out_copy(g):
        rows = pl.ds(g * GROUP, GROUP)
        return pltpu.make_async_copy(out.at[rows], projected.at[rows], out_sem.at[g])

    def store_merged(ref_rows, merged):
        for b in range(4):
            ref_rows(b, merged[b].astype(jnp.bfloat16))

    def relay(g):
        for way in range(2):
            r = 1 + 2 * way
            for copy in early_copies(g, way):
                copy.wait_recv()
            first = g * GROUP + way * HALF
            merged, total = merge(
                [(att[r, first : first + HALF, :], lse[r, g, way]), (early[way, g], early_lse[way, g])]
            )
            for b in range(4):
                att[r, first + b * ROWS : first + (b + 1) * ROWS, :] = merged[b].astype(jnp.bfloat16)
            lse[r, g, way] = total
            for copy in late_copies(g, way, way):
                start(copy)

    def home(g):
        for way in range(2):
            for half in range(2):
                for copy in late_copies(g, way, half):
                    copy.wait_recv()
        row_in_block = lax.broadcasted_iota(jnp.int32, (ROWS, 1), 0)
        for half in range(2):
            first = g * GROUP + half * HALF
            rows = slice(first, first + HALF)
            merged, _ = merge(
                [(att[0, rows, :], lse[0, g, half])]
                + [(late[way, rows, :], late_lse[way, g, half]) for way in range(2)]
            )
            for b in range(4):
                left = query_table[384 + g * 8 + half * 4 + b]
                kept = jnp.where(row_in_block < left, merged[b], 0.0)
                own[0, first + b * ROWS : first + (b + 1) * ROWS, :] = kept.astype(jnp.bfloat16)
        for way in range(2):
            start(y_copy(g, way))

    def pass_on(g):
        for way in range(2):
            y_copy(g, way).wait_recv()
            start(y2_copy(g, way))

    def project(g):
        for way in range(2):
            y2_copy(g, way).wait_recv()
        rows = slice(g * GROUP, (g + 1) * GROUP)

        def columns(n, carry):
            cols = pl.ds(pl.multiple_of(n * 256, 256), 256)
            total = jnp.zeros((GROUP, 256), jnp.float32)
            for r in range(NY):
                depth = pl.ds(pl.multiple_of(((y + r) % NY) * COLS, COLS), COLS)
                total += jnp.dot(own[r, rows, :], w[depth, cols], preferred_element_type=jnp.float32)
            out[rows, cols] = total.astype(jnp.bfloat16)
            return carry

        lax.fori_loop(0, 4, columns, 0)
        out_copy(g).start()

    attend(-1, 0, 2)
    for way in range(2):
        for copy in early_copies(0, way):
            start(copy)
    weight_load.wait()
    for g in range(7):
        if g < 4:
            attend(g, 0 if g < 3 else 2, 8)
            for way in range(2):
                if g < 3:
                    for copy in early_copies(g + 1, way):
                        start(copy)
                for copy in late_copies(g, way, 1 - way):
                    start(copy)
            relay(g)
        if 1 <= g < 5:
            home(g - 1)
        if 2 <= g < 6:
            pass_on(g - 2)
        if 3 <= g:
            project(g - 3)
    for g in range(4):
        out_copy(g).wait()
    for copy in started:
        copy.wait_send()


def body(queries, keys, values, out_weight, dest_slot, pack_slot, seq_start, seq_len):
    total_rows = BLOCKS * ROWS
    tables = lookup_tables(dest_slot, pack_slot, seq_start, seq_len)
    anywhere = pl.BlockSpec(memory_space=pl.ANY)
    smem = pl.BlockSpec(memory_space=pltpu.SMEM)
    bf16, f32, dma = jnp.bfloat16, jnp.float32, pltpu.SemaphoreType.DMA
    projected = pl.pallas_call(
        kernel,
        out_shape=jax.ShapeDtypeStruct((total_rows, out_weight.shape[1]), bf16),
        in_specs=[smem, smem, pl.BlockSpec(memory_space=pltpu.VMEM)] + [anywhere] * 4,
        out_specs=anywhere,
        scratch_shapes=[
            pltpu.VMEM((2, NZ, 2, BLOCKS, ROWS, HEAD_SIZE), bf16),
            pltpu.VMEM((NX, total_rows, COLS), bf16),
            pltpu.VMEM((NX, total_rows, COLS), bf16),
            pltpu.VMEM((NX, 4, 2, 8, HEAD_SIZE), f32),
            pltpu.VMEM((2, 4, HALF, COLS), bf16),
            pltpu.VMEM((2, 4, 8, HEAD_SIZE), f32),
            pltpu.VMEM((2, total_rows, COLS), bf16),
            pltpu.VMEM((2, 4, 2, 8, HEAD_SIZE), f32),
            pltpu.VMEM((NY, total_rows, COLS), bf16),
            pltpu.VMEM(out_weight.shape, bf16),
            pltpu.VMEM((total_rows, out_weight.shape[1]), bf16),
            dma((4,)),
            dma((2, 4, 2)), dma((2, 4, 2)), dma((NZ, 2)), dma((NZ, 2)), dma((2, 6)), dma((2, 6)),
            dma((2, 4)), dma((2, 4)), dma((2, 4)), dma((2, 4)),
            dma((2, 4, 2)), dma((2, 4, 2)), dma((2, 4, 2)), dma((2, 4, 2)),
            dma((2, 4)), dma((2, 4)), dma((2, 4)), dma((2, 4)), dma((4,)),
        ],
        compiler_params=pltpu.CompilerParams(
            collective_id=0, has_side_effects=True, vmem_limit_bytes=60 * 2**20
        ),
    )(
        *tables,
        queries.reshape(total_rows, COLS),
        keys,
        values,
        out_weight,
    )
    return projected.reshape(BLOCKS, ROWS, out_weight.shape[1])


def solution(mesh):
    placed = (
        P("dp", None, "tensor"),
        P("dp", None, "tensor"),
        P("dp", None, "tensor"),
        P(None, "tensor"),
        P("dp"),
        P("dp", None),
        P("dp", None),
        P("dp", None),
    )
    return jax.shard_map(
        body, mesh=mesh, in_specs=placed, out_specs=P("dp", None, "tensor"), check_vma=False
    )
```

time: 253 us -> 174 us (0.69)
  waiting for transfers between devices: 168 us -> 0 us
  Pallas kernels: 0 us -> 119 us
  blocking collectives: 0 us -> 44 us
  starting transfers between devices: 20.1 us -> 0 us
  local copies, waits for them, and re-layouts: 24.2 us -> 6.55 us
  matrix products: 14 us -> 0 us
  between operations: 13.8 us -> 0.1 us
  other arithmetic: 11.5 us -> 3.44 us
    all_to_all x2 -> x0, waiting for transfers between devices: 120 us -> none  [the longest x1 70.5 us: sent_together(): lax.all_to_all(both, axis, split_axis=split_dim, concat_axis=concat_dim,...]
    pallas_call x0 -> x1, Pallas kernels: none -> 119 us  [body(): pl.pallas_call(kernel, out_shape=jax.ShapeDtypeStruct((total_rows, out_we...]
    all_gather x1 -> x0, waiting for transfers between devices: 48.5 us -> none  [body(): lax.all_gather(own_rows, 'tensor', axis=1, tiled=True)]
    all_gather x0 -> x1, blocking collectives: none -> 44 us  [lookup_tables(): table = lax.all_gather(mine, 'dp')]
    all_to_all x2 -> x0, starting transfers between devices: 19.8 us -> none  [the longest x1 13.1 us: sent_together(): lax.all_to_all(both, axis, split_axis=split_dim, concat_axis=concat_dim,...]
    dot_general x7 -> x0, matrix products: 14 us -> none  [the longest x1 9.27 us: body(): jnp.dot(lax.all_gather(own_rows, 'tensor', axis=1, tiled=True), out_weigh...]
    scatter x4 -> x0, local copies, waits for them, and re-layouts: 11.2 us -> none  [the longest x3 6.62 us: outgoing(): jnp.zeros((slot_count,) + portion.shape[1:], portion.dtype).at[dest_slot]]
    gather x4 -> x3, local copies, waits for them, and re-layouts: 7.52 us -> 1.77 us  [the longest x1 0.64 us: lookup_tables(): rows = jnp.take(table, pack, axis=0)]
  transfers between devices with their start and end apart: 3 -> 0, of which waited for: 3 -> 0; matrix products, arithmetic and copies ran while one was open for 1% -> 0% of each run, Pallas kernels for 0% -> 0%
where the time goes in v1:
time: 174 us; the launch traced here: 173 us
  Pallas kernels  119 us (68%)
  blocking collectives  44 us (25%)
  local copies, waits for them, and re-layouts  6.55 us (4%)
  other arithmetic  3.44 us (2%)
    pallas_call x1, Pallas kernels, body(): pl.pallas_call(kernel, out_shape=jax.ShapeDtypeStruct((total_rows, out_we...  119 us
    all_gather x1, blocking collectives, lookup_tables(): table = lax.all_gather(mine, 'dp')  44 us

profile of v1, /device:TPU:1, one launch (start us, length us, event | category | flops | bytes accessed | tf_op | source)
XLA Modules:
  0.0 173.4 jit_solution(18118981141736270032)
XLA Ops:
  0.0 0.8 add_bitcast_fusion
  0.8 0.1 broadcast_add_fusion.1
  0.9 0.1 add.266
  1.0 0.1 add.268
  1.1 0.1 broadcast_in_dim.75
  1.2 0.1 eq.53
  1.3 0.1 add.273
  1.4 44.0 %all-gather.1 = s32[64,1,128]{2,1,0:T(1,128)S(1)} all-gather(s32[1,1,128]{2,1,0:T(1,128)S(1)} %add_bitcast_fusion), channel_id=2, replica_groups=mesh['dp'=64,'tensor'=4] {'dp'}, dimensions={0}, use_global_device_ids=true | all-gather | bytes 33280 | tf_op jit(solution)/shard_map/all_gather | solution.py:23
  45.4 0.1 fusion.20
  45.4 0.6 gather_fusion
  46.0 0.1 broadcast_select_fusion.2
  46.1 0.1 copy.14
  46.1 0.1 select_n.166
  46.2 0.1 select_n.168
  46.3 0.1 compare_reduce_fusion
  46.5 0.1 fusion
  46.6 0.6 gather_fusion.2
  47.2 0.1 broadcast_select_fusion.1
  47.3 0.1 select_reduce_fusion
  47.4 0.1 copy.13
  47.5 0.7 reshape.226.block_table
  48.2 0.6 gather_fusion.1
  48.8 0.1 broadcast_select_fusion
  48.9 0.2 select_reduce_fusion.1
  49.1 0.2 fusion.1
  49.3 0.2 fusion.2
  49.5 0.6 pad_add_fusion.query_table
  50.1 0.1 copy.15
  50.2 0.7 broadcast_add_fusion.key_row
  50.9 119.3 %shard_map.82 = bf16[1024,1024]{1,0:T(8,128)(2,1)} custom-call(s32[416]{0:T(512)} %pad_add_fusion.query_table, s32[1024]{0:T(1024)} %reshape.226.block_table, s32[64,512]{1,0:T(8,128)} %broadcast_add_fusion.key_row, bf16[1024,512]{1,0:T(8,128)(2,1)} %bitcast.19, bf16[32,32,128]{2,1,0:T(8,128)(2,1)} %keys.1, bf16[32,32,128]{2,1,0:T(8,128)(2,1)} %values.1, ...), custom_call_target="tpu_custom_call" | custom-call | tf_op jit(solution)/shard_map/pallas_call | solution.py:353
  170.2 3.2 %copy.17 = bf16[32,32,1024]{2,1,0:T(8,128)(2,1)} copy(bf16[32,32,1024]{2,1,0:T(8,128)(2,1)} %bitcast.18) | data formatting | bytes 4194304
  (16 shorter events, 0.2 us)

commit v2 on v1

--- a/solution.py
+++ b/solution.py
@@ -18,9 +18,42 @@
 LOG2E = 1.4426950408889634
 
 
-def lookup_tables(dest_slot, pack_slot, seq_start, seq_len):
-    mine = jnp.concatenate([dest_slot, pack_slot[0], seq_start[0], seq_len[0]])
-    table = lax.all_gather(mine, "dp")
+N_PACKS = NZ * NX * NC
+ARRIVAL = (0, 1, 7, 2, 6, 3, 5, 4)
+PART = 256
+PIECES = ((0, 6), (6, 14), (14, 22), (22, 24), (24, 32))
+
+
+def heads_down(tile):
+    return jnp.concatenate([tile[:, h * HEAD_SIZE : (h + 1) * HEAD_SIZE] for h in range(4)], axis=0)
+
+
+def heads_across(tile):
+    return jnp.concatenate([tile[h * ROWS : (h + 1) * ROWS] for h in range(4)], axis=1)
+
+
+def diagonal():
+    shape = (HEAD_SIZE, HEAD_SIZE)
+    return lax.broadcasted_iota(jnp.int32, shape, 0) == lax.broadcasted_iota(jnp.int32, shape, 1)
+
+
+def merge(parts):
+    top = functools.reduce(jnp.maximum, [s for _, s in parts])
+    shares = [jnp.exp2(s - top) for _, s in parts]
+    total = functools.reduce(jnp.add, shares)
+    shares = [s / total for s in shares]
+    eye = diagonal()
+    merged = []
+    for b in range(4):
+        weights = jnp.concatenate(
+            [jnp.where(eye, s[b : b + 1], 0.0).astype(jnp.bfloat16) for s in shares], axis=1
+        )
+        outputs = jnp.concatenate([heads_down(o[b * ROWS : (b + 1) * ROWS]) for o, _ in parts], axis=0)
+        merged.append(heads_across(jnp.dot(weights, outputs, preferred_element_type=jnp.float32)))
+    return merged, top + jnp.log2(total)
+
+
+def lookup_tables(table):
     me = lax.axis_index("dp")
     z, x, c = me // (NX * NC), (me // NC) % NX, me % NC
     count = jnp.arange(BLOCKS, dtype=jnp.int32)
@@ -34,8 +67,8 @@
     begin = jnp.max(jnp.where(starts <= place[:, None] * ROWS, starts, 0), axis=1)
     length = jnp.sum(jnp.where(starts == begin[:, None], rows[:, 96:], 0), axis=1)
     left = begin + length - place * ROWS
-    key_z = jnp.tile((z + jnp.arange(NZ)) % NZ, NC)
-    key_c = jnp.repeat((c + jnp.arange(NC)) % NC, NZ)
+    key_z = jnp.repeat((z + jnp.array(ARRIVAL, jnp.int32)) % NZ, NC)
+    key_c = jnp.tile((c + jnp.arange(NC)) % NC, NZ)
     key_loader = (key_z * NX + x) * NC + key_c
     found = sources[:, None, :] == key_loader[None, :, None]
     position = jnp.sum(jnp.where(found, count, 0), axis=2)
@@ -48,46 +81,54 @@
     return query_table, block.reshape(-1).astype(jnp.int32), key_row.astype(jnp.int32)
 
 
-N_PACKS = NZ * NX * NC
-
-
-def heads_down(tile):
-    return jnp.concatenate([tile[:, h * HEAD_SIZE : (h + 1) * HEAD_SIZE] for h in range(4)], axis=0)
-
-
-def heads_across(tile):
-    return jnp.concatenate([tile[h * ROWS : (h + 1) * ROWS] for h in range(4)], axis=1)
-
-
-def diagonal():
-    shape = (HEAD_SIZE, HEAD_SIZE)
-    return lax.broadcasted_iota(jnp.int32, shape, 0) == lax.broadcasted_iota(jnp.int32, shape, 1)
-
-
-def merge(parts):
-    top = functools.reduce(jnp.maximum, [s for _, s in parts])
-    shares = [jnp.exp2(s - top) for _, s in parts]
-    total = functools.reduce(jnp.add, shares)
-    shares = [s / total for s in shares]
-    eye = diagonal()
-    merged = []
-    for b in range(4):
-        weights = jnp.concatenate(
-            [jnp.where(eye, s[b : b + 1], 0.0).astype(jnp.bfloat16) for s in shares], axis=1
-        )
-        outputs = jnp.concatenate([heads_down(o[b * ROWS : (b + 1) * ROWS]) for o, _ in parts], axis=0)
-        merged.append(heads_across(jnp.dot(weights, outputs, preferred_element_type=jnp.float32)))
-    return merged, top + jnp.log2(total)
-
-
-def kernel(
-    query_table, block_table, key_row, queries, keys, values, weight, projected,
-    kv, qx, att, lse, early, early_lse, late, late_lse, own, w, out,
-    local_sem, z_send, z_recv, core_send, core_recv, x_send, x_recv,
-    early_send, early_recv, early_lse_send, early_lse_recv,
-    late_send, late_recv, late_lse_send, late_lse_recv,
-    y_send, y_recv, y2_send, y2_recv, out_sem,
-):
+def share_tables(mine, tab, own_sem, x_send, x_recv, z_send, z_recv):
+    me, y = lax.axis_index("dp"), lax.axis_index("tensor")
+    z, seat = me // 8, me % 8
+    keep = pltpu.make_async_copy(mine, tab.at[pl.ds(me, 1)], own_sem)
+    keep.start()
+    plane = [(z * 8 + (seat + o) % 8, y) for o in range(1, 8)]
+    column = [(((z + o) % NZ) * 8 + seat, y) for o in range(1, 8)]
+    barrier = pltpu.get_barrier_semaphore()
+    for device in plane + column:
+        pl.semaphore_signal(barrier, inc=1, device_id=device, device_id_type=MESH)
+    pl.semaphore_wait(barrier, 14)
+
+    def in_plane(o, row):
+        return pltpu.make_async_remote_copy(
+            src_ref=mine, dst_ref=tab.at[pl.ds(row, 1)], send_sem=x_send.at[o], recv_sem=x_recv.at[o],
+            device_id=plane[o], device_id_type=MESH,
+        )
+
+    def along_z(o, zz):
+        rows = pl.ds(pl.multiple_of(zz * 8, 8), 8)
+        return pltpu.make_async_remote_copy(
+            src_ref=tab.at[rows], dst_ref=tab.at[rows], send_sem=z_send.at[o], recv_sem=z_recv.at[o],
+            device_id=column[o], device_id_type=MESH,
+        )
+
+    for o in range(7):
+        in_plane(o, me).start()
+    keep.wait()
+    for o in range(7):
+        in_plane(o, z * 8 + (seat + 7 - o) % 8).wait_recv()
+    for o in range(7):
+        along_z(o, z).start()
+    for o in range(7):
+        along_z(o, (z + 7 - o) % NZ).wait_recv()
+    for o in range(7):
+        in_plane(o, me).wait_send()
+        along_z(o, z).wait_send()
+
+
+def kernel(query_table, block_table, key_row, queries, keys, values, weight, projected, *scratch):
+    kv = [[scratch[(side * NZ + d) * 2 : (side * NZ + d) * 2 + 2] for d in range(NZ)] for side in range(2)]
+    (
+        packed, qx, first_att, first_lse, att, lse, early, early_lse, late, late_lse, own, w, out,
+        local_sem, z_send, z_recv, core_send, core_recv, x_send, x_recv,
+        early_send, early_recv, early_lse_send, early_lse_recv,
+        late_send, late_recv, late_lse_send, late_lse_recv,
+        y_send, y_recv, y2_send, y2_recv, out_sem,
+    ) = scratch[32:]
     me, y = lax.axis_index("dp"), lax.axis_index("tensor")
     z, x, c = me // (NX * NC), (me // NC) % NX, me % NC
 
@@ -105,8 +146,8 @@
         )
 
     loads = [
-        pltpu.make_async_copy(keys, kv.at[0, 0, 0], local_sem.at[0]),
-        pltpu.make_async_copy(values, kv.at[0, 0, 1], local_sem.at[1]),
+        pltpu.make_async_copy(keys, kv[0][0][0], local_sem.at[0]),
+        pltpu.make_async_copy(values, kv[0][0][1], local_sem.at[1]),
         pltpu.make_async_copy(queries, qx.at[0], local_sem.at[2]),
     ]
     for load in loads:
@@ -131,14 +172,14 @@
         src = (NZ - hop) % NZ if way == 0 else hop
         dst = NZ - hop - 1 if way == 0 else hop + 1
         return remote(
-            kv.at[0, src, t], kv.at[0, dst, t], z_send.at[way, hop, t], z_recv.at[way, hop, t], z_near[way]
+            kv[0][src][t], kv[0][dst][t], z_send.at[way, hop, t], z_recv.at[way, hop, t], z_near[way]
         )
 
     def z_goes(way, hop, t):
         return hop < 3 or (hop == 3 and t == way)
 
     def core_copy(d, t):
-        return remote(kv.at[0, d, t], kv.at[1, d, t], core_send.at[d, t], core_recv.at[d, t], partner)
+        return remote(kv[0][d][t], kv[1][d][t], core_send.at[d, t], core_recv.at[d, t], partner)
 
     def x_copy(way, n):
         g = n if n < 4 else n - 4 + 2 * way
@@ -146,24 +187,95 @@
         rows = pl.ds(g * GROUP, GROUP)
         return remote(qx.at[src, rows], qx.at[dst, rows], x_send.at[way, n], x_recv.at[way, n], x_near[way])
 
-    for t in range(2):
-        for way in range(2):
-            start(z_copy(way, 0, t))
+    def pack(side, d, t):
+        j = ARRIVAL.index(d) * 2 + side
+
+        def step(n, carry):
+            for p in range(8):
+                packed[n * 8 + p, t, j * ROWS : (j + 1) * ROWS, :] = kv[side][d][t][block_table[(n * 8 + p) * 16 + j]]
+            return carry
+
+        lax.fori_loop(0, N_PACKS // 8, step, 0)
+
+    scale = LOG2E / HEAD_SIZE**0.5
+
+    def attend_four(r, g, half, part):
+        base = pl.multiple_of(g * GROUP + half * HALF, HALF)
+        eye = diagonal()
+        row_in_block = lax.broadcasted_iota(jnp.int32, (4 * ROWS, 1), 0) % ROWS
+        keys_of_part = slice(part * PART, (part + 1) * PART)
+        outputs, sums = [], []
+        for b in range(4):
+            n = r * BLOCKS + g * 8 + half * 4 + b
+            to, place, begin = query_table[n], query_table[128 + n], query_table[256 + n]
+            rows = pl.ds(base + b * ROWS, ROWS)
+            q = heads_down(qx[r, rows, :])
+            scores = lax.dot_general(
+                q, packed[to, 0, keys_of_part, :], (((1,), (1,)), ((), ())), preferred_element_type=jnp.float32
+            )
+            key_at = key_row[pl.ds(to, 1), keys_of_part]
+            key_at = jnp.where(key_at >= begin, key_at, FAR)
+            scores = jnp.where(key_at <= place * ROWS + row_in_block, scores * scale, NEG)
+            top = jnp.max(scores, axis=1, keepdims=True)
+            terms = jnp.exp2(scores - top)
+            total = jnp.sum(terms, axis=1, keepdims=True)
+            mixed = jnp.dot(terms.astype(jnp.bfloat16), packed[to, 1, keys_of_part, :], preferred_element_type=jnp.float32)
+            outputs.append(heads_across(mixed / total).astype(jnp.bfloat16))
+            sums.append(jnp.sum(jnp.where(eye, top + jnp.log2(total), 0.0), axis=0, keepdims=True))
+        sums = jnp.concatenate(sums + [jnp.zeros((4, HEAD_SIZE), jnp.float32)], axis=0)
+        if part == 0:
+            for b in range(4):
+                first_att[r, pl.ds(base + b * ROWS, ROWS), :] = outputs[b]
+            first_lse[r, g, half] = sums
+            return
+        merged, sums = merge(
+            [
+                (first_att[r, pl.ds(base, HALF), :], first_lse[r, g, half]),
+                (jnp.concatenate(outputs, axis=0), sums),
+            ]
+        )
+        for b in range(4):
+            att[r, pl.ds(base + b * ROWS, ROWS), :] = merged[b].astype(jnp.bfloat16)
+        lse[r, g, half] = sums
+
+    def attend_first(first, last):
+        def step(u, carry):
+            v = u // 8
+            attend_four(v + v // 2 - 2 * (v // 3), (u % 8) // 2, u % 2, 0)
+            return carry
+
+        lax.fori_loop(first, last, step, 0)
+
+    def pack_all(blocks):
+        for side, d, t in blocks:
+            if side == 1:
+                core_copy(d, t).wait_recv()
+            pack(side, d, t)
+
+    for way in range(2):
+        start(z_copy(way, 0, 0))
     for n in range(4):
         for way in range(2):
             start(x_copy(way, n))
     for t in range(2):
         start(core_copy(0, t))
-
+    for way in range(2):
+        start(z_copy(way, 0, 1))
+    pack_all([(0, 0, 0), (0, 0, 1), (1, 0, 0), (1, 0, 1)])
+
+    arrived = []
     for hop in range(4):
         for t in range(2):
+            due, arrived = arrived, []
             for way in range(2):
                 if not z_goes(way, hop, t):
                     continue
                 z_copy(way, hop, t).wait_recv()
                 if z_goes(way, hop + 1, t):
                     start(z_copy(way, hop + 1, t))
-                start(core_copy(NZ - hop - 1 if way == 0 else hop + 1, t))
+                d = NZ - hop - 1 if way == 0 else hop + 1
+                start(core_copy(d, t))
+                arrived += [(0, d, t), (1, d, t)]
             n = 2 * hop + t
             if n < 4:
                 for way in range(2):
@@ -173,43 +285,17 @@
             elif n < 6:
                 for way in range(2):
                     x_copy(way, n).wait_recv()
-    for d in range(NZ):
-        for t in range(2):
-            core_copy(d, t).wait_recv()
-
-    scale = LOG2E / HEAD_SIZE**0.5
-
-    def attend_four(r, g, half):
-        base = pl.multiple_of(g * GROUP + half * HALF, HALF)
-        eye = diagonal()
-        row_in_block = lax.broadcasted_iota(jnp.int32, (4 * ROWS, 1), 0) % ROWS
-        sums = []
-        for b in range(4):
-            n = r * BLOCKS + g * 8 + half * 4 + b
-            pack, place, begin = query_table[n], query_table[128 + n], query_table[256 + n]
-            rows = pl.ds(base + b * ROWS, ROWS)
-            q = heads_down(qx[r, rows, :])
-            at_block = [block_table[pack * 16 + j] for j in range(16)]
-            key_tile = jnp.concatenate([kv[j // NZ, j % NZ, 0, at_block[j]] for j in range(16)], axis=0)
-            value_tile = jnp.concatenate([kv[j // NZ, j % NZ, 1, at_block[j]] for j in range(16)], axis=0)
-            scores = lax.dot_general(
-                q, key_tile, (((1,), (1,)), ((), ())), preferred_element_type=jnp.float32
-            )
-            key_at = key_row[pl.ds(pack, 1), :]
-            key_at = jnp.where(key_at >= begin, key_at, FAR)
-            scores = jnp.where(key_at <= place * ROWS + row_in_block, scores * scale, NEG)
-            top = jnp.max(scores, axis=1, keepdims=True)
-            terms = jnp.exp2(scores - top)
-            total = jnp.sum(terms, axis=1, keepdims=True)
-            mixed = jnp.dot(terms.astype(jnp.bfloat16), value_tile, preferred_element_type=jnp.float32)
-            att[r, rows, :] = heads_across(mixed / total).astype(jnp.bfloat16)
-            sums.append(jnp.sum(jnp.where(eye, top + jnp.log2(total), 0.0), axis=0, keepdims=True))
-        lse[r, g, half] = jnp.concatenate(sums + [jnp.zeros((4, HEAD_SIZE), jnp.float32)], axis=0)
+            if n == 3:
+                due, arrived = due + sorted(arrived), []
+            pack_all(due)
+            if n >= 3:
+                attend_first(*PIECES[n - 3])
+    pack_all(sorted(arrived))
 
     def attend(g, first, last):
         def step(u, carry):
             v = u // 2
-            attend_four((6 - v) % 4, g + (3 - v) // 3, u % 2)
+            attend_four((6 - v) % 4, g + (3 - v) // 3, u % 2, 1)
             return carry
 
         lax.fori_loop(first, last, step, 0)
@@ -346,18 +432,29 @@
 
 def body(queries, keys, values, out_weight, dest_slot, pack_slot, seq_start, seq_len):
     total_rows = BLOCKS * ROWS
-    tables = lookup_tables(dest_slot, pack_slot, seq_start, seq_len)
+    mine = jnp.concatenate([dest_slot, pack_slot[0], seq_start[0], seq_len[0]])[None]
     anywhere = pl.BlockSpec(memory_space=pl.ANY)
     smem = pl.BlockSpec(memory_space=pltpu.SMEM)
     bf16, f32, dma = jnp.bfloat16, jnp.float32, pltpu.SemaphoreType.DMA
+    table = pl.pallas_call(
+        share_tables,
+        out_shape=jax.ShapeDtypeStruct((N_PACKS, 128), jnp.int32),
+        in_specs=[pl.BlockSpec(memory_space=pltpu.VMEM)],
+        out_specs=pl.BlockSpec(memory_space=pltpu.VMEM),
+        scratch_shapes=[dma(())] + [dma((7,))] * 4,
+        compiler_params=pltpu.CompilerParams(collective_id=1, has_side_effects=True),
+    )(mine)
     projected = pl.pallas_call(
         kernel,
         out_shape=jax.ShapeDtypeStruct((total_rows, out_weight.shape[1]), bf16),
         in_specs=[smem, smem, pl.BlockSpec(memory_space=pltpu.VMEM)] + [anywhere] * 4,
         out_specs=anywhere,
         scratch_shapes=[
-            pltpu.VMEM((2, NZ, 2, BLOCKS, ROWS, HEAD_SIZE), bf16),
+            *[pltpu.VMEM((BLOCKS, ROWS, HEAD_SIZE), bf16)] * 32,
+            pltpu.VMEM((N_PACKS, 2, 16 * ROWS, HEAD_SIZE), bf16),
             pltpu.VMEM((NX, total_rows, COLS), bf16),
+            pltpu.VMEM((NX, total_rows, COLS), bf16),
+            pltpu.VMEM((NX, 4, 2, 8, HEAD_SIZE), f32),
             pltpu.VMEM((NX, total_rows, COLS), bf16),
             pltpu.VMEM((NX, 4, 2, 8, HEAD_SIZE), f32),
             pltpu.VMEM((2, 4, HALF, COLS), bf16),
@@ -377,7 +474,7 @@
             collective_id=0, has_side_effects=True, vmem_limit_bytes=60 * 2**20
         ),
     )(
-        *tables,
+        *lookup_tables(table),
         queries.reshape(total_rows, COLS),
         keys,
         values,

time: 174 us -> 154 us (0.89)
  blocking collectives: 44 us -> 0 us
  Pallas kernels: 119 us -> 141 us
    all_gather x1 -> x0, blocking collectives: 44 us -> none  [lookup_tables(): table = lax.all_gather(mine, 'dp')]
    pallas_call x0 -> x1, Pallas kernels: none -> 17.2 us  [body(): pl.pallas_call(share_tables, out_shape=jax.ShapeDtypeStruct((N_PACKS, 128...]
    pallas_call x1, Pallas kernels: 119 us -> 123 us  [body(): pl.pallas_call(kernel, out_shape=jax.ShapeDtypeStruct((total_rows, out_we...]
where the time goes in v2:
time: 154 us; the launch traced here: 153 us
  Pallas kernels  141 us (92%)
  local copies, waits for them, and re-layouts  8.13 us (5%)
  other arithmetic  4.6 us (3%)
    pallas_call x1, Pallas kernels, body(): pl.pallas_call(kernel, out_shape=jax.ShapeDtypeStruct((total_rows, out_we...  123 us
    pallas_call x1, Pallas kernels, body(): pl.pallas_call(share_tables, out_shape=jax.ShapeDtypeStruct((N_PACKS, 128...  17.2 us
    unnamed x1, local copies, waits for them, and re-layouts  3.19 us

profile of v2, /device:TPU:1, one launch (start us, length us, event | category | flops | bytes accessed | tf_op | source)
XLA Modules:
  0.0 153.4 jit_solution(16533087259704360107)
XLA Ops:
  0.0 0.7 fusion.6
  0.7 1.3 add_bitcast_fusion.mine
  2.0 0.1 broadcast_in_dim.79
  2.1 0.1 eq.53
  2.2 0.1 broadcast_add_fusion.1
  2.2 0.1 add.266
  2.3 0.1 add.268
  2.5 0.1 add.273
  2.5 17.2 %shard_map.91 = s32[64,128]{1,0:T(8,128)} custom-call(s32[1,128]{1,0:T(1,128)} %add_bitcast_fusion.mine), custom_call_target="tpu_custom_call" | custom-call | tf_op jit(solution)/shard_map/pallas_call | solution.py:439
  19.7 0.9 fusion.20
  20.6 0.6 gather_fusion
  21.2 0.1 broadcast_select_fusion.2
  21.3 0.1 copy.12
  21.3 0.1 select_n.166
  21.4 0.1 select_n.168
  21.5 0.1 compare_reduce_fusion
  21.7 0.1 fusion
  21.8 0.6 gather_fusion.2
  22.4 0.1 broadcast_select_fusion.1
  22.5 0.1 select_reduce_fusion
  22.6 0.1 copy.11
  22.7 0.7 reshape.226.block_table
  23.4 1.4 gather_fusion.1
  24.8 0.1 broadcast_select_fusion
  24.9 0.2 select_reduce_fusion.1
  25.1 0.2 fusion.1
  25.2 0.2 fusion.2
  25.5 0.6 pad_add_fusion.query_table
  26.1 0.1 copy.13
  26.2 0.7 broadcast_add_fusion.key_row
  26.9 123.4 %shard_map.92 = bf16[1024,1024]{1,0:T(8,128)(2,1)} custom-call(s32[416]{0:T(512)} %pad_add_fusion.query_table, s32[1024]{0:T(1024)} %reshape.226.block_table, s32[64,512]{1,0:T(8,128)} %broadcast_add_fusion.key_row, bf16[1024,512]{1,0:T(8,128)(2,1)} %bitcast.16, bf16[32,32,128]{2,1,0:T(8,128)(2,1)} %keys.1, bf16[32,32,128]{2,1,0:T(8,128)(2,1)} %values.1, ...), custom_call_target="tpu_custom_call" | custom-call | tf_op jit(solution)/shard_map/pallas_call | solution.py:447
  150.2 3.2 %copy.15 = bf16[32,32,1024]{2,1,0:T(8,128)(2,1)} copy(bf16[32,32,1024]{2,1,0:T(8,128)(2,1)} %bitcast.15) | data formatting | bytes 4194304
  (15 shorter events, 0.1 us)
